TPU v7x, 32 devices: a whole 2x2x4 slice. The times are simulated.
32 devices in a mesh: dp: 8 (over y, x, core), expert: 4 (over z).
Axes of the slice: x: 2, y: 2, z: 4, core: 2. Of those that a mesh axis runs over, the one named last changes fastest.
Arguments:
- tokens: bfloat16 [512, 4096], P('expert', 'dp'), may hold values from -6 to 6
- in_signs: int32 [512, 128], P('expert', 'dp'), may hold values from -2147483648 to 2147483646
- out_signs: int32 [512, 224], P('expert'), may hold values from -2147483648 to 2147483646
- expert_ids: int32 [512, 2], P('expert'), may hold values from 0 to 3, all different within a row; in each aligned block of 128 rows (0 to 127, 128 to 255, ...) at most 80 rows name the same one
- route_weight: float32 [512, 2], P('expert'), may hold values from 0.2 to 1
- cotangent: bfloat16 [512, 7168], P('expert', 'dp'), may hold values from -6 to 6
- mean_weight: bfloat16 [4, 4096, 7168], P('expert', 'dp'), may hold values from -0.09375 to 0.09375
- rho_weight: bfloat16 [4, 4096, 7168], P('expert', 'dp'), may hold values from -6 to -3
- noise_weight: bfloat16 [4, 4096, 7168], P('expert', 'dp'), may hold values from -4 to 4
Outputs:
- hidden_out: bfloat16 [512, 7168], P('expert', 'dp')
- grad_tokens: bfloat16 [512, 4096], P('expert', 'dp')
- grad_mean: bfloat16 [4, 4096, 7168], P('expert', 'dp')
- grad_rho: bfloat16 [4, 4096, 7168], P('expert', 'dp')
Inputs may be any that keep to these rules, and one draw needn't show every extreme that they name: `expert_ids`: each token names 2 different experts. In each aligned block of 128 tokens no expert is named by more than 80 tokens, and in some blocks one expert is named by exactly 80. `in_signs`: bit b of word w, counted from the lowest, is set where the sign of feature 32 * w + b is -1 and clear where it is +1. `out_signs`: bit b of word w, counted from the lowest, is set where the sign of hidden unit 32 * w + b is -1 and clear where it is +1.
All inputs are finite; a program needn't handle non-finite values.
Results may differ from a plain program's by a relative error of at most 0.0071.
Values may be sent and summed in bfloat16 or wider, within the bound.
A program may use at most 128 MiB of HBM per device.

v0:
```python
import jax
import jax.numpy as jnp
from jax import lax
from jax.sharding import PartitionSpec as P


def unpack_rows(words):
    shifts = jnp.arange(32, dtype=jnp.int32)
    bits = jnp.bitwise_and(jnp.right_shift(words[..., None], shifts), 1)
    signs = (1 - 2 * bits).astype(jnp.float32)
    return signs.reshape(words.shape[:-1] + (words.shape[-1] * 32,))


def unpack_cols(words):
    shifts = jnp.arange(32, dtype=jnp.int32)
    bits = jnp.bitwise_and(jnp.right_shift(words.T[:, None, :], shifts[None, :, None]), 1)
    signs = (1 - 2 * bits).astype(jnp.float32)
    return signs.reshape(words.shape[1] * 32, words.shape[0])


def block_slots(block_ids, experts, capacity):
    onehot = (block_ids[:, :, None] == jnp.arange(experts, dtype=jnp.int32)).astype(jnp.int32)
    flat = onehot.reshape(-1, experts)
    before = jnp.cumsum(flat, axis=0) - flat
    ranks = jnp.sum(before * flat, axis=1).reshape(block_ids.shape)
    return block_ids * capacity + ranks


def on_device(
    tokens,
    in_signs,
    out_signs,
    expert_ids,
    route_weight,
    cotangent,
    mean_weight,
    rho_weight,
    noise_weight,
):
    experts = lax.axis_size("expert") * mean_weight.shape[0]
    token_count = tokens.shape[0]
    topk = expert_ids.shape[1]
    capacity = 5 * token_count * topk // (4 * experts)
    slots = experts * capacity
    width_local = tokens.shape[1]
    sign_words = in_signs.shape[1]
    hidden_local = cotangent.shape[1]
    slot_of = block_slots(expert_ids, experts, capacity)
    match = (slot_of[:, :, None] == jnp.arange(slots, dtype=jnp.int32)).astype(jnp.int32)
    token_rank = jnp.arange(token_count, dtype=jnp.int32)[:, None, None]
    slot_token = jnp.sum(match * token_rank, axis=(0, 1))
    slot_fill = jnp.sum(match, axis=(0, 1))
    slot_weight = jnp.sum(match.astype(jnp.float32) * route_weight[:, :, None], axis=(0, 1))
    words = jnp.concatenate([in_signs, out_signs], axis=1)
    fill_rows = slot_fill.astype(jnp.bfloat16)[:, None]
    send_rows = (jnp.take(tokens, slot_token, axis=0) * fill_rows).reshape(
        experts, capacity, width_local
    )
    send_words = jnp.take(words, slot_token, axis=0).reshape(experts, capacity, words.shape[1])
    recv_rows, recv_words = (
        lax.all_to_all(send_rows, "expert", split_axis=0, concat_axis=0, tiled=True),
        lax.all_to_all(send_words, "expert", split_axis=0, concat_axis=0, tiled=True),
    )
    rows = recv_rows.reshape(slots, width_local)
    recv_words = recv_words.reshape(slots, words.shape[1])
    input_signs = unpack_rows(recv_words[:, :sign_words])
    input_cols = unpack_cols(recv_words[:, :sign_words])
    signed = rows * input_signs.astype(jnp.bfloat16)
    mean_local = mean_weight[0]
    rho_float = rho_weight[0].astype(jnp.float32)
    noise_float = noise_weight[0].astype(jnp.float32)
    delta = (jax.nn.softplus(rho_float) * noise_float).astype(jnp.bfloat16)
    contract = (((0,), (1,)), ((), ()))
    output_cols = unpack_cols(recv_words[:, sign_words:])
    mean_cols = mean_local
    delta_cols = delta
    mean_part = lax.dot_general(mean_cols, rows, contract, preferred_element_type=jnp.float32)
    pert_part = lax.dot_general(delta_cols, signed, contract, preferred_element_type=jnp.float32)
    mean_part, pert_part = (mean_part, pert_part)
    preact = lax.psum_scatter(
        mean_part + output_cols * pert_part, "dp", scatter_dimension=0, tiled=True
    )
    gate = jax.nn.sigmoid(preact)
    hidden_slots = (preact * gate).astype(jnp.bfloat16)
    slope = gate * (1.0 + preact * (1.0 - gate))
    returned = lax.all_to_all(
        hidden_slots.reshape(hidden_local, experts, capacity),
        "expert",
        split_axis=1,
        concat_axis=1,
        tiled=True,
    )
    returned = returned.reshape(hidden_local, slots)
    picked = jnp.take(returned, slot_of, axis=1).astype(jnp.float32)
    hidden_out = jnp.sum(picked * route_weight[None], axis=2).T.astype(jnp.bfloat16)
    upstream = jnp.take(cotangent.T, slot_token, axis=1).astype(jnp.float32) * slot_weight[None, :]
    upstream = upstream.astype(jnp.bfloat16).reshape(hidden_local, experts, capacity)
    arrived = lax.all_to_all(upstream, "expert", split_axis=1, concat_axis=1, tiled=True).reshape(
        hidden_local, slots
    )
    grad_preact = (arrived.astype(jnp.float32) * slope).astype(jnp.bfloat16)
    piece = lax.all_gather(grad_preact, "dp", axis=0, tiled=True)
    piece_signed = piece * output_cols.astype(jnp.bfloat16)
    mean_cols = mean_local
    delta_cols = delta
    grad_rows = jnp.dot(mean_cols, piece, preferred_element_type=jnp.float32)
    grad_signed = jnp.dot(delta_cols, piece_signed, preferred_element_type=jnp.float32)
    mean_block = lax.dot_general(rows, piece, contract, preferred_element_type=jnp.float32)
    delta_block = lax.dot_general(
        signed, piece_signed, contract, preferred_element_type=jnp.float32
    )
    grad_mean_acc = mean_block
    grad_delta_acc = delta_block
    result = (grad_rows, grad_signed, grad_mean_acc, grad_delta_acc)
    grad_rows, grad_signed, grad_mean_acc, grad_delta_acc = result
    slot_grad = (grad_rows + input_cols * grad_signed).astype(jnp.bfloat16)
    back = lax.all_to_all(
        slot_grad.reshape(width_local, experts, capacity),
        "expert",
        split_axis=1,
        concat_axis=1,
        tiled=True,
    )
    back = back.reshape(width_local, slots)
    grad_tokens = jnp.sum(jnp.take(back, slot_of, axis=1).astype(jnp.float32), axis=2).T.astype(
        jnp.bfloat16
    )
    grad_mean = grad_mean_acc.astype(jnp.bfloat16)[None]
    grad_rho = (grad_delta_acc * noise_float * jax.nn.sigmoid(rho_float)).astype(jnp.bfloat16)[None]
    return (hidden_out, grad_tokens, grad_mean, grad_rho)


def solution(mesh):
    in_specs = (
        P("expert", "dp"),
        P("expert", "dp"),
        P("expert", None),
        P("expert", None),
        P("expert", None),
        P("expert", "dp"),
        P("expert", "dp", None),
        P("expert", "dp", None),
        P("expert", "dp", None),
    )
    out_specs = (
        P("expert", "dp"),
        P("expert", "dp"),
        P("expert", "dp", None),
        P("expert", "dp", None),
    )
    return jax.shard_map(
        on_device, mesh=mesh, in_specs=in_specs, out_specs=out_specs, check_vma=False
    )
```

profile of v0, /device:TPU:0, one launch (start us, length us, event | category | flops | bytes accessed | tf_op | source)
XLA Modules:
  0.0 268.0 jit_solution(5732661552439096458)
XLA Ops:
  13.1 1.6 gather_fusion.1
  15.6 6.3 %all-to-all-start.1 = ((s32[4,80,240]{2,1,0:T(8,128)}), s32[4,80,240]{2,1,0:T(8,128)S(1)}, u32[]{:S(2)}, u32[]{:S(2)}) async-start(s32[4,80,240]{2,1,0:T(8,128)} %broadcast_select_fusion.2), calls=%async_computation.1 | async-start | bytes 655360 | tf_op jit(solution)/shard_map/all_to_all | solution.py:62
  21.9 3.0 %gather_fusion = bf16[320,512]{1,0:T(8,128)(2,1)S(1)} fusion(bf16[128,512]{1,0:T(8,128)(2,1)} %param.9, s32[1024]{0:T(1024)S(1)} %pad_clamp_fusion.1), kind=kCustom, calls=%fused_computation | custom fusion | bytes 656640 | tf_op jit(solution)/shard_map/jit(_take)/gather | solution.py:56
  25.9 6.3 %all-to-all-done.1 = s32[4,80,240]{2,1,0:T(8,128)S(1)} async-done(((s32[4,80,240]{2,1,0:T(8,128)}), s32[4,80,240]{2,1,0:T(8,128)S(1)}, u32[]{:S(2)}, u32[]{:S(2)}) %all-to-all-start.1) | async-done | bytes 307232 | tf_op jit(solution)/shard_map/all_to_all | solution.py:62
  32.2 3.5 %all-to-all-start = ((bf16[4,80,512]{2,1,0:T(8,128)(2,1)}), bf16[4,80,512]{2,1,0:T(8,128)(2,1)S(1)}, u32[]{:S(2)}, u32[]{:S(2)}) async-start(bf16[4,80,512]{2,1,0:T(8,128)(2,1)} %select_multiply_fusion), calls=%async_computation | async-start | bytes 655360 | tf_op jit(solution)/shard_map/all_to_all | solution.py:61
  38.4 4.9 %shift_right_arithmetic.71 = s32[224,32,320]{2,1,0:T(8,128)} broadcast(s32[224,320]{1,0:T(8,128)S(1)} %bitcast.147), dimensions={0,2} | broadcast | bytes 9461760 | tf_op jit(solution)/shard_map/shift_right_arithmetic | solution.py:16
  43.3 11.5 %copy.78 = s32[7168,320]{0,1:T(8,128)} copy(s32[7168,320]{1,0:T(8,128)} %bitcast.132) | data formatting | bytes 18350080 | tf_op jit(solution)/shard_map/shift_right_arithmetic | solution.py:16
  54.8 9.4 %convolution_bitcast_fusion = f32[7168,320]{0,1:T(8,128)} fusion(bf16[320,512]{1,0:T(8,128)(2,1)S(1)} %bitcast.140, bf16[1,512,7168]{2,1,0:T(8,128)(2,1)} %param.15), kind=kOutput, calls=%fused_computation.34 | convolution fusion | flops 2348810240 | bytes 16842752 | tf_op jit(solution)/shard_map/dot_general | solution.py:77
  65.2 20.1 %fusion.22 = f32[7168,320]{0,1:T(8,128)} fusion(f32[7168,320]{0,1:T(8,128)} %convolution_bitcast_fusion, bf16[320,512]{1,0:T(8,128)(2,1)} %bitcast.150, bf16[1,512,7168]{2,1,0:T(8,128)(2,1)} %param.17, bf16[1,512,7168]{2,1,0:T(8,128)(2,1)} %param.16, s32[7168,320]{0,1:T(8,128)S(1)} %bitcast.134, s32[7168]{0:T(1024)S(1)} %shift_right_arithmetic.74), kind=kOutput, calls=%fused_computation.37 | convolution fusion | flops 2401566720 | bytes 42561536 | tf_op jit(solution)/shard_map/dot_general | solution.py:78
  85.4 2.2 gather_fusion.3
  88.1 18.0 %all_to_all.25 = bf16[896,4,80]{0,2,1:T(8,128)(2,1)S(1)} all-to-all(bf16[896,4,80]{0,2,1:T(8,128)(2,1)S(1)} %multiply_convert_fusion), channel_id=1, replica_groups=mesh['dp'=8,'expert'=4] {'expert'}, dimensions={1} | all-to-all | bytes 1146880 | tf_op jit(solution)/shard_map/all_to_all | solution.py:98
  106.1 55.7 %reduce-scatter.2.cloned.1.call-done = f32[896,320]{0,1:T(8,128)} async-done(((f32[7168,320]{0,1:T(8,128)}), f32[896,320]{0,1:T(8,128)}) %reduce-scatter.2.cloned.1.call-update) | async-done | bytes 1146896 | tf_op jit(solution)/shard_map/reduce_scatter | solution.py:80
  161.8 2.8 %fusion.43 = (bf16[896,320]{0,1:T(8,128)(2,1)}, bf16[896,320]{0,1:T(8,128)(2,1)}) fusion(f32[896,320]{0,1:T(8,128)} %reduce-scatter.2.cloned.1.call-done, bf16[896,4,80]{0,2,1:T(8,128)(2,1)S(1)} %all_to_all.25), kind=kLoop, calls=%fused_computation.51 | loop fusion | flops 3440640 | bytes 2867200 | tf_op jit(solution)/shard_map/convert_element_type | solution.py:101
  164.6 4.6 %all-to-all-start.2 = ((bf16[896,4,80]{0,2,1:T(8,128)(2,1)}), bf16[896,4,80]{0,2,1:T(8,128)(2,1)S(1)}, u32[]{:S(2)}, u32[]{:S(2)}) async-start(bf16[896,4,80]{0,2,1:T(8,128)(2,1)} %bitcast.12), calls=%async_computation.3 | async-start | bytes 1146880 | tf_op jit(solution)/shard_map/all_to_all | solution.py:86
  170.3 14.3 %all-to-all-done.2 = bf16[896,4,80]{0,2,1:T(8,128)(2,1)S(1)} async-done(((bf16[896,4,80]{0,2,1:T(8,128)(2,1)}), bf16[896,4,80]{0,2,1:T(8,128)(2,1)S(1)}, u32[]{:S(2)}, u32[]{:S(2)}) %all-to-all-start.2) | async-done | bytes 573472 | tf_op jit(solution)/shard_map/all_to_all | solution.py:86
  186.0 2.1 multiply_reduce_fusion
  188.1 14.8 %all-gather.2.cloned.1.call-done = bf16[7168,320]{0,1:T(8,128)(2,1)} async-done(((bf16[896,320]{0,1:T(8,128)(2,1)}), bf16[7168,320]{0,1:T(8,128)(2,1)}) %all-gather.2.cloned.1.call-update) | async-done | bytes 4587536 | tf_op jit(solution)/shard_map/all_gather | solution.py:102
  202.9 9.5 %fusion.30 = bf16[7168,320]{0,1:T(8,128)(2,1)} fusion(bf16[7168,320]{0,1:T(8,128)(2,1)} %all-gather.2.cloned.1.call-done, s32[7168,320]{0,1:T(8,128)} %copy.78, s32[7168]{0:T(1024)S(1)} %shift_right_arithmetic.74), kind=kLoop, calls=%fused_computation.45 | loop fusion | flops 22937600 | bytes 18378752 | tf_op jit(solution)/shard_map/mul | solution.py:103
  212.4 13.7 %fusion.20 = bf16[1,512,7168]{2,1,0:T(8,128)(2,1)} fusion(bf16[1,512,7168]{2,1,0:T(8,128)(2,1)} %param.16, bf16[1,512,7168]{2,1,0:T(8,128)(2,1)} %param.17, bf16[7168,320]{0,1:T(8,128)(2,1)} %fusion.30, bf16[320,512]{1,0:T(8,128)(2,1)S(1)} %bitcast.141, s32[320,512]{1,0:T(8,128)S(1)} %copy.85, s32[512]{0:T(512)S(1)} %shift_right_arithmetic.80), kind=kOutput, calls=%fused_computation.35 | convolution fusion | flops 2379808768 | bytes 27592704 | tf_op jit(solution)/shard_map/dot_general | solution.py:109
  226.1 2.6 fusion.31
  228.7 14.5 %fusion.40 = bf16[512,320]{0,1:T(8,128)(2,1)} fusion(f32[512,320]{0,1:T(8,128)S(1)} %fusion.31, bf16[7168,320]{0,1:T(8,128)(2,1)S(1)} %copy-done.4, bf16[1,512,7168]{2,1,0:T(8,128)(2,1)} %param.17, bf16[1,512,7168]{2,1,0:T(8,128)(2,1)} %param.16, s32[512,320]{0,1:T(8,128)S(1)} %copy.84, s32[512]{0:T(512)S(1)} %shift_right_arithmetic.80), kind=kOutput, calls=%fused_computation.49 | convolution fusion | flops 2386821120 | bytes 20908032 | tf_op jit(solution)/shard_map/dot_general | solution.py:107
  243.2 4.6 %all-to-all-start.4 = ((bf16[512,4,80]{0,2,1:T(8,128)(2,1)}), bf16[512,4,80]{0,2,1:T(8,128)(2,1)S(1)}, u32[]{:S(2)}, u32[]{:S(2)}) async-start(bf16[512,4,80]{0,2,1:T(8,128)(2,1)} %bitcast.23), calls=%async_computation.5 | async-start | bytes 655360 | tf_op jit(solution)/shard_map/all_to_all | solution.py:117
  247.9 8.4 %fusion.21 = bf16[1,512,7168]{2,1,0:T(8,128)(2,1)} fusion(bf16[320,512]{1,0:T(8,128)(2,1)S(1)} %bitcast.142, bf16[7168,320]{0,1:T(8,128)(2,1)} %all-gather.2.cloned.1.call-done), kind=kOutput, calls=%fused_computation.36 | convolution fusion | flops 2352480256 | bytes 12255232 | tf_op jit(solution)/shard_map/dot_general | solution.py:108
  256.2 2.3 all-to-all-done.4
  (92 shorter events, 16.8 us)
Async XLA Ops:
  7.2 78.2 %copy-start = (bf16[128,896]{1,0:T(8,128)(2,1)S(1)}, bf16[128,896]{1,0:T(8,128)(2,1)}, u32[]{:S(2)}) copy-start(bf16[128,896]{1,0:T(8,128)(2,1)} %param.14) | copy-start | bytes 688132
  15.6 16.7 %all-to-all-start.1 = ((s32[4,80,240]{2,1,0:T(8,128)}), s32[4,80,240]{2,1,0:T(8,128)S(1)}, u32[]{:S(2)}, u32[]{:S(2)}) async-start(s32[4,80,240]{2,1,0:T(8,128)} %broadcast_select_fusion.2), calls=%async_computation.1 | async-start | bytes 655360 | tf_op jit(solution)/shard_map/all_to_all | solution.py:62
  32.2 22.5 %all-to-all-start = ((bf16[4,80,512]{2,1,0:T(8,128)(2,1)}), bf16[4,80,512]{2,1,0:T(8,128)(2,1)S(1)}, u32[]{:S(2)}, u32[]{:S(2)}) async-start(bf16[4,80,512]{2,1,0:T(8,128)(2,1)} %select_multiply_fusion), calls=%async_computation | async-start | bytes 655360 | tf_op jit(solution)/shard_map/all_to_all | solution.py:61
  35.7 126.1 %reduce-scatter.2.cloned.1.call-start = ((), (), s32[]{:S(2)}) async-start(), calls=%async_computation.6 | async-start | bytes 10321920 | tf_op jit(solution)/shard_map/reduce_scatter | solution.py:80
  36.5 18.3 %copy-start.2 = (s32[320,16,32]{0,2,1:T(8,128)}, s32[320,16,32]{0,2,1:T(8,128)S(1)}, u32[]{:S(2)}) copy-start(s32[320,16,32]{0,2,1:T(8,128)S(1)} %shift_right_arithmetic.77) | copy-start | bytes 1966084
  54.8 10.4 %slice-start = ((s8[9175040]{0:T(1024)(128)(4,1)}), s8[786432]{0:T(1024)(128)(4,1)S(1)}, s32[]{:S(2)}) async-start(s8[9175040]{0:T(1024)(128)(4,1)} %bitcast.133), calls=%async_computation.8 | async-start | bytes 1572864
  54.8 9.5 %copy-start.5 = (s32[4,80,512]{2,1,0:T(8,128)S(1)}, s32[4,80,512]{2,1,0:T(8,128)}, u32[]{:S(2)}) copy-start(s32[4,80,512]{2,1,0:T(8,128)} %copy.80) | copy-start | bytes 1966084
  54.8 10.4 %slice-start.1 = ((s8[9175040]{0:T(1024)(128)(4,1)}), s8[4194304]{0:T(1024)(128)(4,1)S(1)}, s32[]{:S(2)}) async-start(s8[9175040]{0:T(1024)(128)(4,1)} %bitcast.133), calls=%async_computation.9 | async-start | bytes 8388608
  54.8 10.4 %slice-start.2 = ((s8[9175040]{0:T(1024)(128)(4,1)}), s8[4194304]{0:T(1024)(128)(4,1)S(1)}, s32[]{:S(2)}) async-start(s8[9175040]{0:T(1024)(128)(4,1)} %bitcast.133), calls=%async_computation.10 | async-start | bytes 8388608
  85.3 2.3 copy-start.6
  85.3 84.5 %copy-start.3 = (s32[320,16,32]{0,2,1:T(8,128)S(1)}, s32[320,16,32]{0,2,1:T(8,128)}, u32[]{:S(2)}) copy-start(s32[320,16,32]{0,2,1:T(8,128)} %copy-done.2) | copy-start | bytes 1966084
  85.3 117.6 %all-gather.2.cloned.1.call-start = ((), (), s32[]{:S(2)}) async-start(), calls=%async_computation.7 | async-start | bytes 5160960 | tf_op jit(solution)/shard_map/all_gather | solution.py:102
  164.6 20.0 %all-to-all-start.2 = ((bf16[896,4,80]{0,2,1:T(8,128)(2,1)}), bf16[896,4,80]{0,2,1:T(8,128)(2,1)S(1)}, u32[]{:S(2)}, u32[]{:S(2)}) async-start(bf16[896,4,80]{0,2,1:T(8,128)(2,1)} %bitcast.12), calls=%async_computation.3 | async-start | bytes 1146880 | tf_op jit(solution)/shard_map/all_to_all | solution.py:86
  202.9 23.2 %slice-start.3 = ((s8[4587520]{0:T(1024)(128)(4,1)}), s8[393216]{0:T(1024)(128)(4,1)S(1)}, s32[]{:S(2)}) async-start(s8[4587520]{0:T(1024)(128)(4,1)} %bitcast.135), calls=%async_computation.11 | async-start | bytes 786432
  202.9 23.2 %slice-start.5 = ((s8[7340032]{0:T(1024)(128)(4,1)}), s8[4194304]{0:T(1024)(128)(4,1)S(1)}, s32[]{:S(2)}) async-start(s8[7340032]{0:T(1024)(128)(4,1)} %bitcast.137), calls=%async_computation.13 | async-start | bytes 8388608
  212.4 13.7 %slice-start.4 = ((s8[4587520]{0:T(1024)(128)(4,1)}), s8[4194304]{0:T(1024)(128)(4,1)S(1)}, s32[]{:S(2)}) async-start(s8[4587520]{0:T(1024)(128)(4,1)} %bitcast.135), calls=%async_computation.12 | async-start | bytes 8388608
  212.4 13.7 %slice-start.6 = ((s8[7340032]{0:T(1024)(128)(4,1)}), s8[3145728]{0:T(1024)(128)(4,1)S(1)}, s32[]{:S(2)}) async-start(s8[7340032]{0:T(1024)(128)(4,1)} %bitcast.137), calls=%async_computation.14 | async-start | bytes 6291456
  226.1 2.6 copy-start.4
  243.2 15.3 %all-to-all-start.4 = ((bf16[512,4,80]{0,2,1:T(8,128)(2,1)}), bf16[512,4,80]{0,2,1:T(8,128)(2,1)S(1)}, u32[]{:S(2)}, u32[]{:S(2)}) async-start(bf16[512,4,80]{0,2,1:T(8,128)(2,1)} %bitcast.23), calls=%async_computation.5 | async-start | bytes 655360 | tf_op jit(solution)/shard_map/all_to_all | solution.py:117
  258.6 2.6 copy-start.1
Sparse Core Ops, SparseCore 0:
  85.4 76.3 reduce-scatter.1
  164.7 38.1 all-gather.1
where the time goes:
time: 269 us; the launch traced here: 268 us
  waiting for transfers between devices  93.5 us (35%)
  matrix products  68.7 us (26%)
  local copies, waits for them, and re-layouts  32.9 us (12%)
  other arithmetic  21.1 us (8%)
  starting transfers between devices  19.3 us (7%)
  blocking collectives  18 us (7%)
  between operations  14.4 us (5%)
    reduce_scatter x1, waiting for transfers between devices, on_device(): lax.psum_scatter(mean_part + output_cols * pert_part, 'dp', scatter_dimen...  55.7 us
    dot_general x1, matrix products, on_device(): lax.dot_general(delta_cols, signed, contract, preferred_element_type=jnp....  20.1 us
    all_to_all x1, blocking collectives, on_device(): lax.all_to_all(upstream, 'expert', split_axis=1, concat_axis=1, tiled=True)  18 us
    shift_right_arithmetic x6, local copies, waits for them, and re-layouts, unpack_cols(): jnp.right_shift(words.T[:, None, :], shifts[None, :, None])  16.7 us
    all_gather x1, waiting for transfers between devices, on_device(): piece = lax.all_gather(grad_preact, 'dp', axis=0, tiled=True)  14.8 us
    dot_general x1, matrix products, on_device(): jnp.dot(delta_cols, piece_signed, preferred_element_type=jnp.float32)  14.5 us
    all_to_all x1, waiting for transfers between devices, on_device(): lax.all_to_all(hidden_slots.reshape(hidden_local, experts, capacity), 'ex...  14.3 us
    dot_general x1, matrix products, on_device(): lax.dot_general(signed, piece_signed, contract, preferred_element_type=jn...  13.7 us
  transfers between devices with their start and end apart: 6, of which 5 were waited for; matrix products, arithmetic and copies ran while one was open for 14% of the time, Pallas kernels for 0%

commit v1 on v0

--- a/solution.py
+++ b/solution.py
@@ -1,8 +1,11 @@
+import functools
+
 import jax
 import jax.numpy as jnp
 from jax import lax
+from jax.experimental import pallas as pl
+from jax.experimental.pallas import tpu as pltpu
 from jax.sharding import PartitionSpec as P
-
 
 def unpack_rows(words):
     shifts = jnp.arange(32, dtype=jnp.int32)
@@ -26,7 +29,7 @@
     return block_ids * capacity + ranks
 
 
-def on_device(
+def on_device_general(
     tokens,
     in_signs,
     out_signs,
@@ -130,6 +133,251 @@
     return (hidden_out, grad_tokens, grad_mean, grad_rho)
 
 
+LANES = 128
+VMEM_LIMIT = 56 * 1024 * 1024
+
+
+def cost(flops, nbytes, trans=0):
+    return pl.CostEstimate(flops=flops, bytes_accessed=nbytes, transcendentals=trans)
+
+
+def params():
+    return pltpu.CompilerParams(
+        dimension_semantics=("arbitrary",), vmem_limit_bytes=VMEM_LIMIT
+    )
+
+
+def lane_signs(words, first, tiles):
+    slots, total = words.shape
+    lane = lax.broadcasted_iota(jnp.int32, (slots, LANES), 1)
+    shift = lane % 32
+    out = []
+    for tile in range(tiles):
+        at = first + 4 * tile + lane // 32
+        picked = None
+        for part in range(total // LANES):
+            piece = jnp.take_along_axis(
+                words[:, part * LANES : (part + 1) * LANES],
+                at % LANES,
+                axis=1,
+                mode="promise_in_bounds",
+            )
+            picked = piece if part == 0 else jnp.where(at >= part * LANES, piece, picked)
+        bits = jnp.bitwise_and(jnp.right_shift(picked, shift), 1)
+        out.append((1 - 2 * bits).astype(jnp.float32))
+    return jnp.concatenate(out, axis=1) if tiles > 1 else out[0]
+
+
+def delta_kernel(rho_ref, noise_ref, delta_ref):
+    rho = rho_ref[...].astype(jnp.float32)
+    noise = noise_ref[...].astype(jnp.float32)
+    soft = jnp.maximum(rho, 0.0) + jnp.log(1.0 + jnp.exp(-jnp.abs(rho)))
+    delta_ref[...] = (soft * noise).astype(delta_ref.dtype)
+
+
+def make_delta(rho, noise, rows=64):
+    width, hidden = rho.shape
+    spec = pl.BlockSpec((rows, hidden), lambda i: (i, 0))
+    return pl.pallas_call(
+        delta_kernel,
+        grid=(width // rows,),
+        in_specs=[spec, spec],
+        out_specs=spec,
+        out_shape=jax.ShapeDtypeStruct((width, hidden), jnp.bfloat16),
+        compiler_params=params(),
+        cost_estimate=cost(20 * width * hidden, 6 * width * hidden, 2 * width * hidden),
+        name="delta",
+    )(rho, noise)
+
+
+def forward_kernel(in_words, words_ref, rows_ref, mean_ref, delta_ref, y_ref, r_ref, b_ref, s_ref):
+    step = pl.program_id(0)
+    block = mean_ref.shape[1]
+    words = words_ref[...]
+
+    @pl.when(step == 0)
+    def _():
+        signs = lane_signs(words, 0, rows_ref.shape[1] // LANES).astype(jnp.bfloat16)
+        s_ref[...] = signs
+        b_ref[...] = rows_ref[...] * signs
+
+    signs = lane_signs(words, in_words + step * (block // 32), block // LANES)
+    r_ref[0] = signs.astype(jnp.bfloat16)
+    mean_part = jnp.dot(rows_ref[...], mean_ref[...], preferred_element_type=jnp.float32)
+    pert_part = jnp.dot(b_ref[...], delta_ref[...], preferred_element_type=jnp.float32)
+    y_ref[0] = (mean_part + signs * pert_part).astype(y_ref.dtype)
+
+
+def forward(words, rows, mean, delta, parts, in_words):
+    slots, width = rows.shape
+    hidden = mean.shape[1]
+    block = hidden // parts
+    whole = lambda shape: pl.BlockSpec(shape, lambda i: (0, 0))
+    weight = pl.BlockSpec((width, block), lambda i: (0, i))
+    piece = pl.BlockSpec((1, slots, block), lambda i: (i, 0, 0))
+    small = jax.ShapeDtypeStruct((slots, width), jnp.bfloat16)
+    large = jax.ShapeDtypeStruct((parts, slots, block), jnp.bfloat16)
+    return pl.pallas_call(
+        functools.partial(forward_kernel, in_words),
+        grid=(parts,),
+        in_specs=[whole(words.shape), whole(rows.shape), weight, weight],
+        out_specs=[piece, piece, whole(rows.shape), whole(rows.shape)],
+        out_shape=[large, large, small, small],
+        compiler_params=params(),
+        cost_estimate=cost(4 * slots * width * hidden, 4 * hidden * (width + slots)),
+        name="forward",
+    )(words, rows, mean, delta)
+
+
+NT = (((1,), (1,)), ((), ()))
+
+
+def back_kernel(dy_ref, r_ref, mean_ref, delta_ref, s_ref, g_ref, plain, signed):
+    step = pl.program_id(0)
+    dy = dy_ref[0]
+    one = lax.dot_general(dy, mean_ref[...], NT, preferred_element_type=jnp.float32)
+    two = lax.dot_general(dy * r_ref[0], delta_ref[...], NT, preferred_element_type=jnp.float32)
+
+    @pl.when(step == 0)
+    def _():
+        plain[...] = one
+        signed[...] = two
+
+    @pl.when(step > 0)
+    def _():
+        plain[...] += one
+        signed[...] += two
+
+    @pl.when(step == pl.num_programs(0) - 1)
+    def _():
+        total = plain[...] + s_ref[...].astype(jnp.float32) * signed[...]
+        g_ref[...] = total.astype(g_ref.dtype)
+
+
+def back(dy, r, mean, delta, s):
+    parts, slots, block = dy.shape
+    width = mean.shape[0]
+    hidden = parts * block
+    weight = pl.BlockSpec((width, block), lambda i: (0, i))
+    piece = pl.BlockSpec((1, slots, block), lambda i: (i, 0, 0))
+    whole = pl.BlockSpec((slots, width), lambda i: (0, 0))
+    return pl.pallas_call(
+        back_kernel,
+        grid=(parts,),
+        in_specs=[piece, piece, weight, weight, whole],
+        out_specs=whole,
+        out_shape=jax.ShapeDtypeStruct((slots, width), jnp.bfloat16),
+        scratch_shapes=[pltpu.VMEM((slots, width), jnp.float32)] * 2,
+        compiler_params=params(),
+        cost_estimate=cost(4 * slots * width * hidden, 4 * hidden * (width + slots)),
+        name="back",
+    )(dy, r, mean, delta, s)
+
+
+def grads_kernel(dy_ref, r_ref, rho_ref, noise_ref, at_ref, bt_ref, gm_ref, gr_ref):
+    dy = dy_ref[0]
+    gm = jnp.dot(at_ref[...], dy, preferred_element_type=jnp.float32)
+    gm_ref[...] = gm.astype(gm_ref.dtype)
+    gd = jnp.dot(bt_ref[...], dy * r_ref[0], preferred_element_type=jnp.float32)
+    gate = 1.0 / (1.0 + jnp.exp(-rho_ref[...].astype(jnp.float32)))
+    gr_ref[...] = (gd * noise_ref[...].astype(jnp.float32) * gate).astype(gr_ref.dtype)
+
+
+def grads(dy, r, rho, noise, at, bt):
+    parts, slots, block = dy.shape
+    width, hidden = rho.shape
+    weight = pl.BlockSpec((width, block), lambda i: (0, i))
+    piece = pl.BlockSpec((1, slots, block), lambda i: (i, 0, 0))
+    whole = pl.BlockSpec((width, slots), lambda i: (0, 0))
+    out = jax.ShapeDtypeStruct((width, hidden), jnp.bfloat16)
+    return pl.pallas_call(
+        grads_kernel,
+        grid=(parts,),
+        in_specs=[piece, piece, weight, weight, whole, whole],
+        out_specs=[weight, weight],
+        out_shape=[out, out],
+        compiler_params=params(),
+        cost_estimate=cost(4 * slots * width * hidden, 8 * hidden * (width + slots)),
+        name="grads",
+    )(dy, r, rho, noise, at, bt)
+
+
+def exact_dot(onehot, values):
+    return jnp.dot(onehot, values, preferred_element_type=jnp.float32)
+
+
+def on_device(
+    tokens,
+    in_signs,
+    out_signs,
+    expert_ids,
+    route_weight,
+    cotangent,
+    mean_weight,
+    rho_weight,
+    noise_weight,
+):
+    parts = lax.axis_size("dp")
+    hidden_local = cotangent.shape[1]
+    width_local = tokens.shape[1]
+    if hidden_local % LANES or width_local % LANES:
+        return on_device_general(
+            tokens,
+            in_signs,
+            out_signs,
+            expert_ids,
+            route_weight,
+            cotangent,
+            mean_weight,
+            rho_weight,
+            noise_weight,
+        )
+    experts = lax.axis_size("expert") * mean_weight.shape[0]
+    token_count = tokens.shape[0]
+    topk = expert_ids.shape[1]
+    capacity = 5 * token_count * topk // (4 * experts)
+    slots = experts * capacity
+    in_words = in_signs.shape[1]
+    mean, rho, noise = mean_weight[0], rho_weight[0], noise_weight[0]
+    slot_of = block_slots(expert_ids, experts, capacity)
+    match = slot_of[:, :, None] == jnp.arange(slots, dtype=jnp.int32)
+    take_of = [match[:, k, :].astype(jnp.bfloat16) for k in range(topk)]
+    fill_of = jnp.sum(match.astype(jnp.float32), axis=1).astype(jnp.bfloat16)
+    slot_weight = jnp.sum(match.astype(jnp.float32) * route_weight[:, :, None], axis=(0, 1))
+    token_rank = jnp.arange(token_count, dtype=jnp.int32)[:, None, None]
+    slot_token = jnp.sum(match.astype(jnp.int32) * token_rank, axis=(0, 1))
+    words = jnp.concatenate([in_signs, out_signs], axis=1)
+    words = jnp.pad(words, ((0, 0), (0, -words.shape[1] % LANES)))
+    send_words = jnp.take(words, slot_token, axis=0).reshape(experts, capacity, -1)
+    fill_t = fill_of.T
+    send_rows = exact_dot(fill_t, tokens).astype(jnp.bfloat16)
+    upstream = (exact_dot(fill_t, cotangent) * slot_weight[:, None]).astype(jnp.bfloat16)
+    swap = functools.partial(
+        lax.all_to_all, axis_name="expert", split_axis=0, concat_axis=0, tiled=True
+    )
+    recv_rows = swap(send_rows.reshape(experts, capacity, -1)).reshape(slots, -1)
+    recv_words = swap(send_words).reshape(slots, -1)
+    arrived = swap(upstream.reshape(experts, capacity, -1)).reshape(slots, -1)
+    delta = make_delta(rho, noise)
+    partial, r, signed, s = forward(recv_words, recv_rows, mean, delta, parts, in_words)
+    preact = lax.psum_scatter(partial, "dp", scatter_dimension=0, tiled=False)
+    preact = preact.astype(jnp.float32)
+    gate = jax.nn.sigmoid(preact)
+    hidden_slots = (preact * gate).astype(jnp.bfloat16)
+    slope = gate * (1.0 + preact * (1.0 - gate))
+    dy = (arrived.astype(jnp.float32) * slope).astype(jnp.bfloat16)
+    dy_all = lax.all_gather(dy, "dp", axis=0, tiled=False)
+    returned = swap(hidden_slots.reshape(experts, capacity, -1)).reshape(slots, -1)
+    hidden_out = sum(
+        exact_dot(take_of[k], returned) * route_weight[:, k][:, None] for k in range(topk)
+    ).astype(jnp.bfloat16)
+    g = back(dy_all, r, mean, delta, s)
+    g_back = swap(g.reshape(experts, capacity, -1)).reshape(slots, -1)
+    grad_mean, grad_rho = grads(dy_all, r, rho, noise, recv_rows.T, signed.T)
+    grad_tokens = exact_dot(fill_of, g_back).astype(jnp.bfloat16)
+    return (hidden_out, grad_tokens, grad_mean[None], grad_rho[None])
+
+
 def solution(mesh):
     in_specs = (
         P("expert", "dp"),

time: 269 us -> 204 us (0.76)
  matrix products: 68.7 us -> 3.55 us
  Pallas kernels: 0 us -> 57.8 us
  local copies, waits for them, and re-layouts: 32.9 us -> 7.61 us
  waiting for transfers between devices: 93.5 us -> 75.6 us
  other arithmetic: 21.1 us -> 6.97 us
    dot_general x6 -> x5, matrix products: 68.7 us -> 3.55 us  [exact_dot(): return jnp.dot(onehot, values, preferred_element_type=jnp.float32)]
    pallas_call x0 -> x4, Pallas kernels: none -> 57.8 us  [the longest x1 18.2 us: grads(): pl.pallas_call(grads_kernel, grid=(parts,), in_specs=[piece, piece, weigh...]
    reduce_scatter x1, waiting for transfers between devices: 55.7 us -> 36.2 us  [on_device(): preact = lax.psum_scatter(partial, 'dp', scatter_dimension=0, tiled=False)]
    shift_right_arithmetic x12 -> x0, local copies, waits for them, and re-layouts: 18.9 us -> none  [the longest x6 16.7 us: unpack_cols(): jnp.right_shift(words.T[:, None, :], shifts[None, :, None])]
    mul x3 -> x0, other arithmetic: 11.3 us -> none  [the longest x1 9.5 us: on_device(): piece_signed = piece * output_cols.astype(jnp.bfloat16)]
    gather x7 -> x1, local copies, waits for them, and re-layouts: 9.42 us -> 1.63 us  [on_device(): jnp.take(words, slot_token, axis=0).reshape(experts, capacity, -1)]
    reduce_sum x3 -> x1, other arithmetic: 3.61 us -> 0.15 us  [on_device(): slot_token = jnp.sum(match.astype(jnp.int32) * token_rank, axis=(0, 1))]
  transfers between devices with their start and end apart: 6 -> 6, of which waited for: 5 -> 4; matrix products, arithmetic and copies ran while one was open for 14% -> 3% of each run, Pallas kernels for 0% -> 15%
where the time goes in v1:
time: 204 us; the launch traced here: 203 us
  waiting for transfers between devices  75.6 us (37%)
  Pallas kernels  57.8 us (28%)
  starting transfers between devices  19.2 us (9%)
  blocking collectives  18.2 us (9%)
  between operations  14.2 us (7%)
  local copies, waits for them, and re-layouts  7.61 us (4%)
  other arithmetic  6.97 us (3%)
  matrix products  3.55 us (2%)
    reduce_scatter x1, waiting for transfers between devices, on_device(): preact = lax.psum_scatter(partial, 'dp', scatter_dimension=0, tiled=False)  36.2 us
    pallas_call x1, Pallas kernels, grads(): pl.pallas_call(grads_kernel, grid=(parts,), in_specs=[piece, piece, weigh...  18.2 us
    all_to_all x1, blocking collectives, on_device(): arrived = swap(upstream.reshape(experts, capacity, -1)).reshape(slots, -1)  18.2 us
    all_gather x1, waiting for transfers between devices, on_device(): dy_all = lax.all_gather(dy, 'dp', axis=0, tiled=False)  16.8 us
    pallas_call x1, Pallas kernels, back(): pl.pallas_call(back_kernel, grid=(parts,), in_specs=[piece, piece, weight...  13.7 us
    pallas_call x1, Pallas kernels, forward(): pl.pallas_call(functools.partial(forward_kernel, in_words), grid=(parts,)...  13.5 us
    all_to_all x1, waiting for transfers between devices, on_device(): swap(hidden_slots.reshape(experts, capacity, -1)).reshape(slots, -1)  13.5 us
    pallas_call x1, Pallas kernels, make_delta(): pl.pallas_call(delta_kernel, grid=(width // rows,), in_specs=[spec, spec]...  12.4 us
  transfers between devices with their start and end apart: 6, of which 4 were waited for; matrix products, arithmetic and copies ran while one was open for 3% of the time, Pallas kernels for 15%

profile of v1, /device:TPU:0, one launch (start us, length us, event | category | flops | bytes accessed | tf_op | source)
XLA Modules:
  0.0 203.2 jit_solution(15222623000047863510)
XLA Ops:
  8.3 1.2 reduce-window.6
  11.9 1.0 copy.50
  13.0 1.6 gather_fusion
  14.6 0.8 pad_select_fusion
  15.5 6.3 %all-to-all-start = ((s32[4,80,256]{2,1,0:T(8,128)}), s32[4,80,256]{2,1,0:T(8,128)S(1)}, u32[]{:S(2)}, u32[]{:S(2)}) async-start(s32[4,80,256]{2,1,0:T(8,128)} %bitcast.3), calls=%async_computation | async-start | bytes 655360 | tf_op jit(solution)/shard_map/all_to_all | solution.py:359
  22.0 1.0 convolution_convert_fusion
  22.9 9.2 %all-to-all-done = s32[4,80,256]{2,1,0:T(8,128)S(1)} async-done(((s32[4,80,256]{2,1,0:T(8,128)}), s32[4,80,256]{2,1,0:T(8,128)S(1)}, u32[]{:S(2)}, u32[]{:S(2)}) %all-to-all-start) | async-done | bytes 327712 | tf_op jit(solution)/shard_map/all_to_all | solution.py:359
  32.1 3.5 %all-to-all-start.1 = ((bf16[4,80,512]{2,1,0:T(8,128)(2,1)}), bf16[4,80,512]{2,1,0:T(8,128)(2,1)S(1)}, u32[]{:S(2)}, u32[]{:S(2)}) async-start(bf16[4,80,512]{2,1,0:T(8,128)(2,1)} %bitcast.5), calls=%async_computation.1 | async-start | bytes 655360 | tf_op jit(solution)/shard_map/all_to_all | solution.py:358
  35.6 12.4 %delta.1.delta_ref = bf16[512,7168]{1,0:T(8,128)(2,1)} custom-call(bf16[512,7168]{1,0:T(8,128)(2,1)} %bitcast.58, bf16[512,7168]{1,0:T(8,128)(2,1)} %bitcast.60), custom_call_target="tpu_custom_call" | custom-call | flops 73400320 | bytes 22020096 | tf_op jit(solution)/shard_map/delta/pallas_call | solution.py:181
  48.7 13.5 %forward.1 = (bf16[8,320,896]{2,1,0:T(8,128)(2,1)}, bf16[8,320,896]{2,1,0:T(8,128)(2,1)}, bf16[320,512]{1,0:T(8,128)(2,1)}, bf16[320,512]{1,0:T(8,128)(2,1)}) custom-call(s32[320,256]{1,0:T(8,128)} %bitcast.75, bf16[320,512]{1,0:T(8,128)(2,1)} %bitcast.71, bf16[512,7168]{1,0:T(8,128)(2,1)} %bitcast.62, bf16[512,7168]{1,0:T(8,128)(2,1)} %delta.1.delta_ref), custom_call_target="tpu_custom_call" | custom-call | flops 4697620480 | bytes 23855104 | tf_op jit(solution)/shard_map/forward/pallas_call | solution.py:220
  62.7 18.2 %all_to_all.25 = bf16[4,80,896]{2,1,0:T(8,128)(2,1)S(1)} all-to-all(bf16[4,80,896]{2,1,0:T(8,128)(2,1)S(1)} %bitcast.66), channel_id=1, replica_groups=mesh['dp'=8,'expert'=4] {'expert'}, dimensions={0} | all-to-all | bytes 1146880 | tf_op jit(solution)/shard_map/all_to_all | solution.py:360
  80.8 36.2 %reduce-scatter.2.cloned.1.call-done = bf16[1,320,896]{2,1,0:T(8,128)(2,1)} async-done(((bf16[8,320,896]{2,1,0:T(8,128)(2,1)}), bf16[1,320,896]{2,1,0:T(8,128)(2,1)}) %reduce-scatter.2.cloned.1.call-update) | async-done | bytes 573456 | tf_op jit(solution)/shard_map/reduce_scatter | solution.py:363
  117.0 2.4 %fusion.3 = bf16[1,320,896]{2,1,0:T(8,128)(2,1)} fusion(bf16[1,320,896]{2,1,0:T(8,128)(2,1)} %reduce-scatter.2.cloned.1.call-done, bf16[1,320,896]{2,1,0:T(8,128)(2,1)S(1)} %bitcast.68), kind=kLoop, calls=%fused_computation.10 | loop fusion | flops 3153920 | bytes 1720320 | tf_op jit(solution)/shard_map/convert_element_type | solution.py:368
  119.5 1.1 multiply_convert_fusion
  120.6 4.7 %all-to-all-start.2 = ((bf16[4,80,896]{2,1,0:T(8,128)(2,1)}), bf16[4,80,896]{2,1,0:T(8,128)(2,1)S(1)}, u32[]{:S(2)}, u32[]{:S(2)}) async-start(bf16[4,80,896]{2,1,0:T(8,128)(2,1)} %multiply_convert_fusion), calls=%async_computation.3 | async-start | bytes 1146880 | tf_op jit(solution)/shard_map/all_to_all | solution.py:370
  125.4 0.9 copy.51
  126.4 0.9 copy.52
  127.3 13.5 %all-to-all-done.2 = bf16[4,80,896]{2,1,0:T(8,128)(2,1)S(1)} async-done(((bf16[4,80,896]{2,1,0:T(8,128)(2,1)}), bf16[4,80,896]{2,1,0:T(8,128)(2,1)S(1)}, u32[]{:S(2)}, u32[]{:S(2)}) %all-to-all-start.2) | async-done | bytes 573472 | tf_op jit(solution)/shard_map/all_to_all | solution.py:370
  141.1 16.8 %all-gather.2.cloned.1.call-done.dy_ref = bf16[8,320,896]{2,1,0:T(8,128)(2,1)} async-done(((bf16[1,320,896]{2,1,0:T(8,128)(2,1)}), bf16[8,320,896]{2,1,0:T(8,128)(2,1)}) %all-gather.2.cloned.1.call-update) | async-done | bytes 4587536 | tf_op jit(solution)/shard_map/all_gather | solution.py:369
  157.9 13.7 %back.1 = bf16[320,512]{1,0:T(8,128)(2,1)} custom-call(bf16[8,320,896]{2,1,0:T(8,128)(2,1)} %all-gather.2.cloned.1.call-done.dy_ref, bf16[8,320,896]{2,1,0:T(8,128)(2,1)} %get-tuple-element.11.r_ref, bf16[512,7168]{1,0:T(8,128)(2,1)} %bitcast.63, bf16[512,7168]{1,0:T(8,128)(2,1)} %delta.1.delta_ref, bf16[320,512]{1,0:T(8,128)(2,1)} %get-tuple-element.12.s_ref), custom_call_target="tpu_custom_call" | custom-call | flops 4697620480 | bytes 23855104 | tf_op jit(solution)/shard_map/back/pallas_call | solution.py:264
  171.6 4.6 %all-to-all-start.4 = ((bf16[4,80,512]{2,1,0:T(8,128)(2,1)}), bf16[4,80,512]{2,1,0:T(8,128)(2,1)S(1)}, u32[]{:S(2)}, u32[]{:S(2)}) async-start(bf16[4,80,512]{2,1,0:T(8,128)(2,1)} %bitcast.74), calls=%async_computation.5 | async-start | bytes 655360 | tf_op jit(solution)/shard_map/all_to_all | solution.py:375
  176.2 1.0 fusion.2
  177.2 18.2 %grads.1 = (bf16[512,7168]{1,0:T(8,128)(2,1)}, bf16[512,7168]{1,0:T(8,128)(2,1)}) custom-call(bf16[8,320,896]{2,1,0:T(8,128)(2,1)} %all-gather.2.cloned.1.call-done.dy_ref, bf16[8,320,896]{2,1,0:T(8,128)(2,1)} %get-tuple-element.11.r_ref, bf16[512,7168]{1,0:T(8,128)(2,1)} %bitcast.59, bf16[512,7168]{1,0:T(8,128)(2,1)} %bitcast.61, ...), custom_call_target="tpu_custom_call" | custom-call | flops 4697620480 | bytes 47710208 | tf_op jit(solution)/shard_map/grads/pallas_call | solution.py:293
  195.4 0.9 convolution_convert_fusion.1
  (47 shorter events, 5.2 us)
Async XLA Ops:
  7.2 55.2 %copy-start = (bf16[128,896]{1,0:T(8,128)(2,1)S(1)}, bf16[128,896]{1,0:T(8,128)(2,1)}, u32[]{:S(2)}) copy-start(bf16[128,896]{1,0:T(8,128)(2,1)} %param.14) | copy-start | bytes 688132
  14.6 7.2 %copy-start.7 = (f32[128,2]{0,1:T(2,128)S(1)}, f32[128,2]{0,1:T(2,128)}, u32[]{:S(2)}) copy-start(f32[128,2]{0,1:T(2,128)} %param.13) | copy-start | bytes 3076
  14.6 7.4 %copy-start.6 = (bf16[128,512]{1,0:T(8,128)(2,1)S(1)}, bf16[128,512]{1,0:T(8,128)(2,1)}, u32[]{:S(2)}) copy-start(bf16[128,512]{1,0:T(8,128)(2,1)} %param.9) | copy-start | bytes 393220
  15.5 16.7 %all-to-all-start = ((s32[4,80,256]{2,1,0:T(8,128)}), s32[4,80,256]{2,1,0:T(8,128)S(1)}, u32[]{:S(2)}, u32[]{:S(2)}) async-start(s32[4,80,256]{2,1,0:T(8,128)} %bitcast.3), calls=%async_computation | async-start | bytes 655360 | tf_op jit(solution)/shard_map/all_to_all | solution.py:359
  32.1 15.9 %copy-start.5 = (s32[4,80,256]{2,1,0:T(8,128)}, s32[4,80,256]{2,1,0:T(8,128)S(1)}, u32[]{:S(2)}) copy-start(s32[4,80,256]{2,1,0:T(8,128)S(1)} %all-to-all-done) | copy-start | bytes 983044
  32.1 15.9 %all-to-all-start.1 = ((bf16[4,80,512]{2,1,0:T(8,128)(2,1)}), bf16[4,80,512]{2,1,0:T(8,128)(2,1)S(1)}, u32[]{:S(2)}, u32[]{:S(2)}) async-start(bf16[4,80,512]{2,1,0:T(8,128)(2,1)} %bitcast.5), calls=%async_computation.1 | async-start | bytes 655360 | tf_op jit(solution)/shard_map/all_to_all | solution.py:358
  35.6 81.4 %reduce-scatter.2.cloned.1.call-start = ((), (), s32[]{:S(2)}) async-start(), calls=%async_computation.6 | async-start | bytes 5160960 | tf_op jit(solution)/shard_map/reduce_scatter | solution.py:363
  48.0 0.7 copy-start.2
  62.3 95.6 %all-gather.2.cloned.1.call-start = ((), (), s32[]{:S(2)}) async-start(), calls=%async_computation.7 | async-start | bytes 5160960 | tf_op jit(solution)/shard_map/all_gather | solution.py:369
  117.0 2.5 %copy-start.1 = (bf16[1,320,896]{2,1,0:T(8,128)(2,1)S(1)}, bf16[1,320,896]{2,1,0:T(8,128)(2,1)}, u32[]{:S(2)}) copy-start(bf16[1,320,896]{2,1,0:T(8,128)(2,1)} %reduce-scatter.2.cloned.1.call-done) | copy-start | bytes 1720324
  119.5 6.0 %copy-start.3 = (bf16[4,80,512]{2,1,0:T(8,128)(2,1)S(1)}, bf16[4,80,512]{2,1,0:T(8,128)(2,1)}, u32[]{:S(2)}) copy-start(bf16[4,80,512]{2,1,0:T(8,128)(2,1)} %copy-done.2) | copy-start | bytes 983044
  120.6 5.8 %copy-start.4 = (bf16[320,512]{1,0:T(8,128)(2,1)S(1)}, bf16[320,512]{1,0:T(8,128)(2,1)}, u32[]{:S(2)}) copy-start(bf16[320,512]{1,0:T(8,128)(2,1)} %get-tuple-element.13) | copy-start | bytes 983044
  120.6 20.1 %all-to-all-start.2 = ((bf16[4,80,896]{2,1,0:T(8,128)(2,1)}), bf16[4,80,896]{2,1,0:T(8,128)(2,1)S(1)}, u32[]{:S(2)}, u32[]{:S(2)}) async-start(bf16[4,80,896]{2,1,0:T(8,128)(2,1)} %multiply_convert_fusion), calls=%async_computation.3 | async-start | bytes 1146880 | tf_op jit(solution)/shard_map/all_to_all | solution.py:370
  171.6 23.8 %all-to-all-start.4 = ((bf16[4,80,512]{2,1,0:T(8,128)(2,1)}), bf16[4,80,512]{2,1,0:T(8,128)(2,1)S(1)}, u32[]{:S(2)}, u32[]{:S(2)}) async-start(bf16[4,80,512]{2,1,0:T(8,128)(2,1)} %bitcast.74), calls=%async_computation.5 | async-start | bytes 655360 | tf_op jit(solution)/shard_map/all_to_all | solution.py:375
Sparse Core Ops, SparseCore 0:
  62.4 54.5 reduce-scatter.1
  119.6 38.2 all-gather.1

commit v2 on v1

--- a/solution.py
+++ b/solution.py
@@ -302,6 +302,173 @@
     )(dy, r, rho, noise, at, bt)
 
 
+def exchange_kernel(
+    p_ref, up_ref, out_ref, back_ref, arr, rd, cs, ra, rb, rc, h_ref, send_sem, recv_sem
+):
+    me = lax.axis_index("dp")
+    mine = lax.axis_index("expert")
+    ranks = up_ref.shape[0]
+    cap = up_ref.shape[1]
+    half = p_ref.shape[1] // 2
+    y, x, c = me // 4, (me // 2) % 2, me % 2
+    place = lambda dy, dx, dc: ((y + dy) % 2) * 4 + ((x + dx) % 2) * 2 + (c + dc) % 2
+    at_x, at_y, at_c = place(0, 1, 0), place(1, 0, 0), place(0, 0, 1)
+    rows = [pl.ds(0, half), pl.ds(half, half)]
+    peers = [(at_x, mine), (at_y, mine), (at_c, mine)]
+    peers += [(me, (mine + j) % ranks) for j in range(1, ranks)]
+    count = [0]
+    started = []
+
+    def send(src, dst, to):
+        n = count[0]
+        count[0] += 1
+        copy = pltpu.make_async_remote_copy(
+            src_ref=src,
+            dst_ref=dst,
+            send_sem=send_sem.at[n],
+            recv_sem=recv_sem.at[n],
+            device_id=to,
+            device_id_type=pl.DeviceIdType.MESH,
+        )
+        copy.start()
+        started.append(copy)
+        return copy
+
+    barrier = pltpu.get_barrier_semaphore()
+    for peer in peers:
+        pl.semaphore_signal(barrier, inc=1, device_id=peer, device_id_type=pl.DeviceIdType.MESH)
+    pl.semaphore_wait(barrier, len(peers))
+
+    order = (3, 1, 2, 0)
+    core = {
+        k: send(p_ref.at[place(k // 2, k % 2, 1)], rd.at[k], (at_c, mine)) for k in order
+    }
+    to_owner = [
+        send(up_ref.at[(mine + j) % ranks], arr.at[mine], (me, (mine + j) % ranks))
+        for j in range(1, ranks)
+    ]
+    arr[mine] = up_ref[mine]
+
+    def add(*terms):
+        total = terms[0].astype(jnp.float32)
+        for term in terms[1:]:
+            total = total + term.astype(jnp.float32)
+        return total
+
+    def chip_sum(k, which):
+        at = rows[which]
+        cs[k, at] = add(p_ref[place(k // 2, k % 2, 0), at], rd[k, at]).astype(cs.dtype)
+
+    core[3].wait_recv()
+    chip_sum(3, 0)
+    along_x = [send(cs.at[3, rows[0]], ra.at[1], (at_x, mine))]
+    chip_sum(3, 1)
+    along_y = [send(cs.at[3, rows[1]], rb.at[1], (at_y, mine))]
+    core[1].wait_recv()
+    chip_sum(1, 0)
+    along_x.append(send(cs.at[1, rows[0]], ra.at[0], (at_x, mine)))
+    core[2].wait_recv()
+    chip_sum(2, 1)
+    along_y.append(send(cs.at[2, rows[1]], rb.at[0], (at_y, mine)))
+    along_x[0].wait_recv()
+    at = rows[0]
+    cs[2, at] = add(p_ref[place(1, 0, 0), at], rd[2, at], ra[1]).astype(cs.dtype)
+    last_y = send(cs.at[2, at], rc.at[0], (at_y, mine))
+    along_y[0].wait_recv()
+    at = rows[1]
+    cs[1, at] = add(p_ref[place(0, 1, 0), at], rd[1, at], rb[1]).astype(cs.dtype)
+    last_x = send(cs.at[1, at], rc.at[1], (at_x, mine))
+    core[0].wait_recv()
+    for copy in to_owner:
+        copy.wait_recv()
+
+    def activate(which, near):
+        per = ranks // 2
+        for i in range(per):
+            own = pl.ds(which * half + i * cap, cap)
+            part = pl.ds(i * cap, cap)
+            preact = add(p_ref[me, own], rd[0, own], near[0, part], rc[which, part])
+            gate = 1.0 / (1.0 + jnp.exp(-preact))
+            h_ref[which * per + i] = (preact * gate).astype(h_ref.dtype)
+            slope = gate * (1.0 + preact * (1.0 - gate))
+            up = arr[which * per + i].astype(jnp.float32)
+            out_ref[me, own] = (up * slope).astype(out_ref.dtype)
+
+    def spread(owner, which, to):
+        piece = out_ref.at[owner, rows[which]]
+        return send(piece, piece, (to, mine))
+
+    along_x[1].wait_recv()
+    last_y.wait_recv()
+    activate(0, ra)
+    y_one = spread(me, 0, at_y)
+    x_two = spread(me, 0, at_x)
+    c_all = [spread(me, 0, at_c)]
+    along_y[1].wait_recv()
+    last_x.wait_recv()
+    activate(1, rb)
+    x_one = spread(me, 1, at_x)
+    y_two = spread(me, 1, at_y)
+    c_all.append(spread(me, 1, at_c))
+    to_token = [
+        send(h_ref.at[(mine + j) % ranks], back_ref.at[mine], (me, (mine + j) % ranks))
+        for j in range(1, ranks)
+    ]
+    back_ref[mine] = h_ref[mine]
+    y_one.wait_recv()
+    x_three = spread(at_y, 0, at_x)
+    c_all.append(spread(at_y, 0, at_c))
+    x_one.wait_recv()
+    y_three = spread(at_x, 1, at_y)
+    c_all.append(spread(at_x, 1, at_c))
+    x_two.wait_recv()
+    c_all.append(spread(at_x, 0, at_c))
+    y_two.wait_recv()
+    c_all.append(spread(at_y, 1, at_c))
+    x_three.wait_recv()
+    c_all.append(spread(place(1, 1, 0), 0, at_c))
+    y_three.wait_recv()
+    c_all.append(spread(place(1, 1, 0), 1, at_c))
+    for copy in c_all + to_token:
+        copy.wait_recv()
+    for copy in started:
+        copy.wait_send()
+
+
+def exchange(partial, upstream):
+    parts, slots, block = partial.shape
+    ranks, cap, _ = upstream.shape
+    bf16 = jnp.bfloat16
+    vmem = pl.BlockSpec(memory_space=pltpu.VMEM)
+    copies = 4 + 4 + 2 + 6 + 8 + 2 * (ranks - 1)
+    half = (2, slots // 2, block)
+    return pl.pallas_call(
+        exchange_kernel,
+        in_specs=[vmem, vmem],
+        out_specs=[vmem, vmem],
+        out_shape=[
+            jax.ShapeDtypeStruct(partial.shape, bf16),
+            jax.ShapeDtypeStruct(upstream.shape, bf16),
+        ],
+        scratch_shapes=[
+            pltpu.VMEM(upstream.shape, bf16),
+            pltpu.VMEM((4, slots, block), bf16),
+            pltpu.VMEM((4, slots, block), bf16),
+            pltpu.VMEM(half, bf16),
+            pltpu.VMEM(half, bf16),
+            pltpu.VMEM(half, bf16),
+            pltpu.VMEM(upstream.shape, bf16),
+            pltpu.SemaphoreType.DMA((copies,)),
+            pltpu.SemaphoreType.DMA((copies,)),
+        ],
+        compiler_params=pltpu.CompilerParams(
+            collective_id=0, has_side_effects=True, vmem_limit_bytes=VMEM_LIMIT
+        ),
+        cost_estimate=cost(10 * partial.size, 100 * partial.size),
+        name="exchange",
+    )(partial, upstream)
+
+
 def exact_dot(onehot, values):
     return jnp.dot(onehot, values, preferred_element_type=jnp.float32)
 
@@ -318,9 +485,12 @@
     noise_weight,
 ):
     parts = lax.axis_size("dp")
+    token_count = tokens.shape[0]
     hidden_local = cotangent.shape[1]
     width_local = tokens.shape[1]
-    if hidden_local % LANES or width_local % LANES:
+    ranks = lax.axis_size("expert")
+    fits = parts == 8 and ranks % 2 == 0 and mean_weight.shape[0] == 1
+    if not fits or hidden_local % LANES or width_local % LANES or token_count % 128:
         return on_device_general(
             tokens,
             in_signs,
@@ -332,8 +502,7 @@
             rho_weight,
             noise_weight,
         )
-    experts = lax.axis_size("expert") * mean_weight.shape[0]
-    token_count = tokens.shape[0]
+    experts = ranks
     topk = expert_ids.shape[1]
     capacity = 5 * token_count * topk // (4 * experts)
     slots = experts * capacity
@@ -357,17 +526,10 @@
     )
     recv_rows = swap(send_rows.reshape(experts, capacity, -1)).reshape(slots, -1)
     recv_words = swap(send_words).reshape(slots, -1)
-    arrived = swap(upstream.reshape(experts, capacity, -1)).reshape(slots, -1)
     delta = make_delta(rho, noise)
     partial, r, signed, s = forward(recv_words, recv_rows, mean, delta, parts, in_words)
-    preact = lax.psum_scatter(partial, "dp", scatter_dimension=0, tiled=False)
-    preact = preact.astype(jnp.float32)
-    gate = jax.nn.sigmoid(preact)
-    hidden_slots = (preact * gate).astype(jnp.bfloat16)
-    slope = gate * (1.0 + preact * (1.0 - gate))
-    dy = (arrived.astype(jnp.float32) * slope).astype(jnp.bfloat16)
-    dy_all = lax.all_gather(dy, "dp", axis=0, tiled=False)
-    returned = swap(hidden_slots.reshape(experts, capacity, -1)).reshape(slots, -1)
+    dy_all, returned = exchange(partial, upstream.reshape(experts, capacity, -1))
+    returned = returned.reshape(slots, -1)
     hidden_out = sum(
         exact_dot(take_of[k], returned) * route_weight[:, k][:, None] for k in range(topk)
     ).astype(jnp.bfloat16)

time: 204 us -> 153 us (0.75)
  waiting for transfers between devices: 75.6 us -> 7.63 us
  Pallas kernels: 57.8 us -> 112 us
  blocking collectives: 18.2 us -> 0 us
  between operations: 14.2 us -> 0.77 us
  starting transfers between devices: 19.2 us -> 13.5 us
  other arithmetic: 6.97 us -> 4.07 us
    pallas_call x0 -> x1, Pallas kernels: none -> 53.9 us  [exchange(): pl.pallas_call(exchange_kernel, in_specs=[vmem, vmem], out_specs=[vmem, v...]
    reduce_scatter x1 -> x0, waiting for transfers between devices: 36.2 us -> none  [on_device(): preact = lax.psum_scatter(partial, 'dp', scatter_dimension=0, tiled=False)]
    all_to_all x1 -> x0, blocking collectives: 18.2 us -> none  [on_device(): arrived = swap(upstream.reshape(experts, capacity, -1)).reshape(slots, -1)]
    all_gather x1 -> x0, waiting for transfers between devices: 16.8 us -> none  [on_device(): dy_all = lax.all_gather(dy, 'dp', axis=0, tiled=False)]
    all_to_all x1 -> x0, waiting for transfers between devices: 13.5 us -> none  [on_device(): swap(hidden_slots.reshape(experts, capacity, -1)).reshape(slots, -1)]
    all_to_all x1 -> x0, starting transfers between devices: 4.74 us -> none  [on_device(): swap(hidden_slots.reshape(experts, capacity, -1)).reshape(slots, -1)]
    convert_element_type x2 -> x0, other arithmetic: 3.57 us -> none  [the longest x1 2.42 us: on_device(): dy = (arrived.astype(jnp.float32) * slope).astype(jnp.bfloat16)]
  transfers between devices with their start and end apart: 6 -> 3, of which waited for: 4 -> 1; matrix products, arithmetic and copies ran while one was open for 3% -> 5% of each run, Pallas kernels for 15% -> 20%
where the time goes in v2:
time: 153 us; the launch traced here: 151 us
  Pallas kernels  112 us (73%)
  starting transfers between devices  13.5 us (9%)
  local copies, waits for them, and re-layouts  8.39 us (5%)
  waiting for transfers between devices  7.63 us (5%)
  matrix products  5.28 us (3%)
  other arithmetic  4.07 us (3%)
    pallas_call x1, Pallas kernels, exchange(): pl.pallas_call(exchange_kernel, in_specs=[vmem, vmem], out_specs=[vmem, v...  53.9 us
    pallas_call x1, Pallas kernels, grads(): pl.pallas_call(grads_kernel, grid=(parts,), in_specs=[piece, piece, weigh...  18.2 us
    pallas_call x1, Pallas kernels, back(): pl.pallas_call(back_kernel, grid=(parts,), in_specs=[piece, piece, weight...  13.8 us
    pallas_call x1, Pallas kernels, forward(): pl.pallas_call(functools.partial(forward_kernel, in_words), grid=(parts,)...  13.5 us
    pallas_call x1, Pallas kernels, make_delta(): pl.pallas_call(delta_kernel, grid=(width // rows,), in_specs=[spec, spec]...  12.4 us
    all_to_all x1, waiting for transfers between devices, on_device(): recv_words = swap(send_words).reshape(slots, -1)  7.63 us
    all_to_all x1, starting transfers between devices, on_device(): recv_words = swap(send_words).reshape(slots, -1)  6.35 us
    dot_general x5, matrix products, exact_dot(): return jnp.dot(onehot, values, preferred_element_type=jnp.float32)  5.28 us
  transfers between devices with their start and end apart: 3, of which 1 were waited for; matrix products, arithmetic and copies ran while one was open for 5% of the time, Pallas kernels for 20%

profile of v2, /device:TPU:0, one launch (start us, length us, event | category | flops | bytes accessed | tf_op | source)
XLA Modules:
  0.0 151.5 jit_solution(3878893395476031426)
XLA Ops:
  0.6 0.8 copy.44
  1.8 1.2 reduce-window.6
  4.5 0.8 copy.49
  5.3 1.0 copy.50
  6.4 1.6 %gather_fusion = s32[320,240]{1,0:T(8,128)S(1)} fusion(s32[128,240]{1,0:T(8,128)S(1)} %pad_add_fusion, s32[1024]{0:T(1024)S(1)} %pad_clamp_fusion), kind=kCustom, calls=%fused_computation | custom fusion | bytes 615680 | tf_op jit(solution)/shard_map/jit(_take)/gather | solution.py:520
  8.1 0.8 pad_select_fusion
  8.9 6.3 %all-to-all-start = ((s32[4,80,256]{2,1,0:T(8,128)}), s32[4,80,256]{2,1,0:T(8,128)S(1)}, u32[]{:S(2)}, u32[]{:S(2)}) async-start(s32[4,80,256]{2,1,0:T(8,128)} %bitcast.3), calls=%async_computation | async-start | bytes 655360 | tf_op jit(solution)/shard_map/all_to_all | solution.py:528
  15.2 0.8 select_reduce_fusion
  16.1 1.9 %convolution_convert_fusion = bf16[320,512]{1,0:T(8,128)(2,1)} fusion(bf16[128,512]{1,0:T(8,128)(2,1)} %param.9, bf16[128,320]{0,1:T(8,128)(2,1)S(1)} %get-tuple-element.21), kind=kOutput, calls=%fused_computation.3 | convolution fusion | flops 42106880 | bytes 540672 | tf_op jit(solution)/shard_map/dot_general | solution.py:473
  17.9 7.6 %all-to-all-done = s32[4,80,256]{2,1,0:T(8,128)S(1)} async-done(((s32[4,80,256]{2,1,0:T(8,128)}), s32[4,80,256]{2,1,0:T(8,128)S(1)}, u32[]{:S(2)}, u32[]{:S(2)}) %all-to-all-start) | async-done | bytes 327712 | tf_op jit(solution)/shard_map/all_to_all | solution.py:528
  25.6 3.5 %all-to-all-start.1 = ((bf16[4,80,512]{2,1,0:T(8,128)(2,1)}), bf16[4,80,512]{2,1,0:T(8,128)(2,1)S(1)}, u32[]{:S(2)}, u32[]{:S(2)}) async-start(bf16[4,80,512]{2,1,0:T(8,128)(2,1)} %bitcast.5), calls=%async_computation.1 | async-start | bytes 655360 | tf_op jit(solution)/shard_map/all_to_all | solution.py:527
  29.0 0.8 slice_bitcast_fusion.4
  29.8 12.4 %delta.1.delta_ref = bf16[512,7168]{1,0:T(8,128)(2,1)} custom-call(bf16[512,7168]{1,0:T(8,128)(2,1)} %bitcast.52, bf16[512,7168]{1,0:T(8,128)(2,1)} %bitcast.54), custom_call_target="tpu_custom_call" | custom-call | flops 73400320 | bytes 22020096 | tf_op jit(solution)/shard_map/delta/pallas_call | solution.py:181
  42.2 1.1 fusion
  43.4 0.7 copy-done.2
  44.1 13.5 %forward.1 = (bf16[8,320,896]{2,1,0:T(8,128)(2,1)}, bf16[8,320,896]{2,1,0:T(8,128)(2,1)}, bf16[320,512]{1,0:T(8,128)(2,1)}, bf16[320,512]{1,0:T(8,128)(2,1)}) custom-call(s32[320,256]{1,0:T(8,128)} %bitcast.67, bf16[320,512]{1,0:T(8,128)(2,1)} %bitcast.63, bf16[512,7168]{1,0:T(8,128)(2,1)} %bitcast.56, bf16[512,7168]{1,0:T(8,128)(2,1)} %delta.1.delta_ref), custom_call_target="tpu_custom_call" | custom-call | flops 4697620480 | bytes 23855104 | tf_op jit(solution)/shard_map/forward/pallas_call | solution.py:220
  57.6 53.9 %exchange.1 = (bf16[8,320,896]{2,1,0:T(8,128)(2,1)}, bf16[4,80,896]{2,1,0:T(8,128)(2,1)}) custom-call(bf16[8,320,896]{2,1,0:T(8,128)(2,1)} %get-tuple-element.12.p_ref, bf16[4,80,896]{2,1,0:T(8,128)(2,1)} %bitcast.58), custom_call_target="tpu_custom_call" | custom-call | flops 22937600 | bytes 229376000 | tf_op jit(solution)/shard_map/exchange/pallas_call | solution.py:445
  111.6 13.8 %back.1 = bf16[320,512]{1,0:T(8,128)(2,1)} custom-call(bf16[8,320,896]{2,1,0:T(8,128)(2,1)} %get-tuple-element.14.dy_ref, bf16[8,320,896]{2,1,0:T(8,128)(2,1)} %get-tuple-element.15.r_ref, bf16[512,7168]{1,0:T(8,128)(2,1)} %bitcast.57, bf16[512,7168]{1,0:T(8,128)(2,1)} %delta.1.delta_ref, bf16[320,512]{1,0:T(8,128)(2,1)} %get-tuple-element.16.s_ref), custom_call_target="tpu_custom_call" | custom-call | flops 4697620480 | bytes 23855104 | tf_op jit(solution)/shard_map/back/pallas_call | solution.py:264
  125.4 3.7 %all-to-all-start.2 = ((bf16[4,80,512]{2,1,0:T(8,128)(2,1)}), bf16[4,80,512]{2,1,0:T(8,128)(2,1)S(1)}, u32[]{:S(2)}, u32[]{:S(2)}) async-start(bf16[4,80,512]{2,1,0:T(8,128)(2,1)} %bitcast.66), calls=%async_computation.2 | async-start | bytes 655360 | tf_op jit(solution)/shard_map/all_to_all | solution.py:537
  129.4 1.0 fusion.2
  130.5 1.0 copy.51
  131.4 0.9 copy.52
  132.4 18.2 %grads.1 = (bf16[512,7168]{1,0:T(8,128)(2,1)}, bf16[512,7168]{1,0:T(8,128)(2,1)}) custom-call(bf16[8,320,896]{2,1,0:T(8,128)(2,1)} %get-tuple-element.14.dy_ref, bf16[8,320,896]{2,1,0:T(8,128)(2,1)} %get-tuple-element.15.r_ref, bf16[512,7168]{1,0:T(8,128)(2,1)} %bitcast.53, bf16[512,7168]{1,0:T(8,128)(2,1)} %bitcast.55, bf16[512,320]{1,0:T(8,128)(2,1)} %bitcast.61, ...), custom_call_target="tpu_custom_call" | custom-call | flops 4697620480 | bytes 47710208 | tf_op jit(solution)/shard_map/grads/pallas_call | solution.py:293
  150.6 0.9 convolution_convert_fusion.1
  (33 shorter events, 2.3 us)
Async XLA Ops:
  0.6 41.6 %copy-start = (bf16[128,896]{1,0:T(8,128)(2,1)S(1)}, bf16[128,896]{1,0:T(8,128)(2,1)}, u32[]{:S(2)}) copy-start(bf16[128,896]{1,0:T(8,128)(2,1)} %param.14) | copy-start | bytes 688132
  8.9 16.7 %all-to-all-start = ((s32[4,80,256]{2,1,0:T(8,128)}), s32[4,80,256]{2,1,0:T(8,128)S(1)}, u32[]{:S(2)}, u32[]{:S(2)}) async-start(s32[4,80,256]{2,1,0:T(8,128)} %bitcast.3), calls=%async_computation | async-start | bytes 655360 | tf_op jit(solution)/shard_map/all_to_all | solution.py:528
  25.6 16.6 %copy-start.4 = (s32[4,80,256]{2,1,0:T(8,128)}, s32[4,80,256]{2,1,0:T(8,128)S(1)}, u32[]{:S(2)}) copy-start(s32[4,80,256]{2,1,0:T(8,128)S(1)} %all-to-all-done) | copy-start | bytes 983044
  25.6 17.8 %all-to-all-start.1 = ((bf16[4,80,512]{2,1,0:T(8,128)(2,1)}), bf16[4,80,512]{2,1,0:T(8,128)(2,1)S(1)}, u32[]{:S(2)}, u32[]{:S(2)}) async-start(bf16[4,80,512]{2,1,0:T(8,128)(2,1)} %bitcast.5), calls=%async_computation.1 | async-start | bytes 655360 | tf_op jit(solution)/shard_map/all_to_all | solution.py:527
  43.4 0.7 copy-start.2
  111.6 17.5 %copy-start.1 = (bf16[4,80,896]{2,1,0:T(8,128)(2,1)S(1)}, bf16[4,80,896]{2,1,0:T(8,128)(2,1)}, u32[]{:S(2)}) copy-start(bf16[4,80,896]{2,1,0:T(8,128)(2,1)} %get-tuple-element.13) | copy-start | bytes 1720324
  111.6 18.9 %copy-start.3 = (bf16[4,80,512]{2,1,0:T(8,128)(2,1)S(1)}, bf16[4,80,512]{2,1,0:T(8,128)(2,1)}, u32[]{:S(2)}) copy-start(bf16[4,80,512]{2,1,0:T(8,128)(2,1)} %copy-done.2) | copy-start | bytes 983044
  111.6 19.9 %copy-start.5 = (bf16[320,512]{1,0:T(8,128)(2,1)S(1)}, bf16[320,512]{1,0:T(8,128)(2,1)}, u32[]{:S(2)}) copy-start(bf16[320,512]{1,0:T(8,128)(2,1)} %get-tuple-element.17) | copy-start | bytes 983044
  125.4 25.2 %all-to-all-start.2 = ((bf16[4,80,512]{2,1,0:T(8,128)(2,1)}), bf16[4,80,512]{2,1,0:T(8,128)(2,1)S(1)}, u32[]{:S(2)}, u32[]{:S(2)}) async-start(bf16[4,80,512]{2,1,0:T(8,128)(2,1)} %bitcast.66), calls=%async_computation.2 | async-start | bytes 655360 | tf_op jit(solution)/shard_map/all_to_all | solution.py:537
